TPU v7x, 32 devices: a whole 2x2x4 slice. The times are simulated.
32 devices in a mesh: gx: 4 (over z), gy: 2 (over y), gz: 4 (over x, core).
Axes of the slice: x: 2, y: 2, z: 4, core: 2. Of those that a mesh axis runs over, the one named last changes fastest.
Arguments:
- colloc: bfloat16 [768, 4000], P(('gx', 'gy')), may hold values from -6 to 6
- occ_coeffs: bfloat16 [4000, 1024], P(None, 'gz'), may hold values from -0.09375 to 0.09375
- core: bfloat16 [768, 2, 384], P('gx', 'gy'), may hold values from -6.246567e-05 to 6.246567e-05
Outputs:
- coulomb: float32 [96, 4000], P(('gx', 'gz'), 'gy')
- exchange: float32 [96, 4000], P(('gx', 'gz'), 'gy')
All inputs are finite; a program needn't handle non-finite values.
Results may differ from a plain program's by a relative error of at most 0.0089.
Values may be sent and summed in bfloat16 or wider, within the bound.
A program may use at most 64 MiB of HBM per device.

v0:
```python
import jax
import jax.numpy as jnp
from jax import lax
from jax.sharding import PartitionSpec as P

W = 96


def local(colloc, occ_coeffs, core):
    points, width = colloc.shape
    size_x = lax.axis_size("gx")
    size_y = lax.axis_size("gy")
    size_z = lax.axis_size("gz")
    row_count = core.shape[0]
    flat_cols = core.shape[2]
    col_points = flat_cols // size_x
    per_rows = W // (size_x * size_z)
    occ_vals = jnp.dot(colloc, occ_coeffs, preferred_element_type=jnp.float32).astype(jnp.bfloat16)
    window_vals = colloc[:, :W].reshape(points, size_x, size_z, per_rows)
    window_vals = window_vals.transpose(0, 2, 1, 3).reshape(points, size_z, size_x * per_rows)
    column_vals = lax.all_gather(occ_vals, "gx", axis=0, tiled=True)
    square_part = jnp.sum(jnp.square(column_vals.astype(jnp.float32)), axis=1)
    density = lax.psum(square_part, "gz").astype(jnp.bfloat16)
    core_flat = core.reshape(row_count, flat_cols)
    potential_rows = jnp.dot(core_flat, density, preferred_element_type=jnp.float32)
    potential = lax.psum_scatter(potential_rows, "gy", scatter_dimension=0, tiled=True)
    occ_piece = lax.all_gather(occ_vals, "gy", axis=0, tiled=True)
    win_piece = lax.all_gather(window_vals, "gy", axis=0, tiled=True)
    count = occ_piece.shape[0]
    gram = lax.dot_general(
        occ_piece, column_vals, (((1,), (1,)), ((), ())), preferred_element_type=jnp.float32
    )
    mixed = (core_flat.astype(jnp.float32) * gram).astype(jnp.bfloat16)
    mixed = mixed.reshape(count, size_x, col_points)
    totals = jnp.einsum("rap,rgk->agpk", mixed, win_piece, preferred_element_type=jnp.float32)
    weighted = (window_vals.astype(jnp.float32) * potential[:, None, None]).astype(jnp.bfloat16)
    x_cols = colloc.reshape(points, size_y, width // size_y)
    group = lax.axis_index("gz")
    owned = lax.psum_scatter(
        totals.reshape(size_x * size_z, col_points, size_x * per_rows),
        ("gx", "gz"),
        scatter_dimension=0,
        tiled=True,
    )
    owned = owned[0].astype(jnp.bfloat16)
    mine = lax.dynamic_index_in_dim(weighted, group, 1, keepdims=False)
    coul = jnp.einsum(
        "pbk,pcj->bckj",
        mine.reshape(points, size_x, per_rows),
        x_cols,
        preferred_element_type=jnp.float32,
    )
    exch = jnp.einsum(
        "pbk,pcj->bckj",
        owned.reshape(points, size_x, per_rows),
        x_cols,
        preferred_element_type=jnp.float32,
    )
    coul = coul.reshape(size_x * size_y, per_rows, width // size_y)
    exch = exch.reshape(size_x * size_y, per_rows, width // size_y)
    coul, exch = (
        lax.psum_scatter(coul, ("gx", "gy"), scatter_dimension=0, tiled=True),
        lax.psum_scatter(exch, ("gx", "gy"), scatter_dimension=0, tiled=True),
    )
    coulomb = coul[0]
    exchange = exch[0]
    return (coulomb, exchange)


def solution(mesh):
    in_specs = (P(("gx", "gy"), None), P(None, "gz"), P("gx", "gy", None))
    out_specs = (P(("gx", "gz"), "gy"), P(("gx", "gz"), "gy"))
    return jax.shard_map(local, mesh=mesh, in_specs=in_specs, out_specs=out_specs, check_vma=False)
```

profile of v0, /device:TPU:0, one launch (start us, length us, event | category | flops | bytes accessed | tf_op | source)
XLA Modules:
  0.0 231.2 jit_solution(8461250890403525931)
XLA Ops:
  7.2 0.0 copy-start
  7.2 0.0 slice-start
  7.2 0.0 copy-start.1
  7.2 0.0 reduce-scatter.10.cloned.1.call-start
  7.2 1.5 copy-done
  8.7 1.6 convolution_convert_fusion
  10.3 15.5 %all_gather.9 = bf16[384,256]{1,0:T(8,128)(2,1)S(1)} all-gather(bf16[96,256]{1,0:T(8,128)(2,1)S(1)} %convolution_convert_fusion), channel_id=1, replica_groups=mesh['gx'=4,'gy'=2,'gz'=4] {'gx'}, dimensions={0}, use_global_device_ids=true | all-gather | bytes 245760 | tf_op jit(solution)/shard_map/all_gather | solution.py:21
  25.8 4.7 %all_gather.10 = bf16[192,256]{1,0:T(8,128)(2,1)S(1)} all-gather(bf16[96,256]{1,0:T(8,128)(2,1)S(1)} %convolution_convert_fusion), channel_id=1, replica_groups=mesh['gx'=4,'gy'=2,'gz'=4] {'gy'}, dimensions={0}, use_global_device_ids=true | all-gather | bytes 147456 | tf_op jit(solution)/shard_map/all_gather | solution.py:27
  30.6 0.0 slice-done
  30.6 0.1 copy.15
  30.7 0.0 copy-done.1
  30.7 0.0 copy-start.2
  30.7 0.2 fusion
  31.0 0.1 reshape.42
  31.1 0.1 copy.18
  31.3 5.3 %all_gather.11 = bf16[192,4,24]{2,1,0:T(4,128)(2,1)S(1)} all-gather(bf16[96,4,24]{2,1,0:T(4,128)(2,1)S(1)} %copy.18), channel_id=1, replica_groups=mesh['gx'=4,'gy'=2,'gz'=4] {'gy'}, dimensions={0}, use_global_device_ids=true | all-gather | bytes 55296 | tf_op jit(solution)/shard_map/all_gather | solution.py:28
  36.6 0.1 copy.20
  36.7 0.9 fusion.7
  37.6 0.0 reduce-scatter.10.cloned.1.call-update
  37.6 0.0 reduce-scatter.6.cloned.1.call-start
  37.6 0.1 multiply_reduce_fusion
  37.8 2.9 %reshape.40 = bf16[96,2,2000]{2,1,0:T(2,128)(2,1)S(1)} reshape(bf16[96,4000]{1,0:T(8,128)(2,1)} %param.3) | data formatting | bytes 1536000 | tf_op jit(solution)/shard_map/reshape | solution.py:37
  40.7 5.7 %psum.7 = bf16[384]{0:T(512)(128)(2,1)S(1)} all-reduce(f32[384]{0:T(512)S(1)} %multiply_reduce_fusion), channel_id=1, replica_groups=mesh['gx'=4,'gy'=2,'gz'=4] {'gz'}, use_global_device_ids=true, to_apply=%region_1.0 | all-reduce | flops 384 | bytes 2304 | tf_op jit(solution)/shard_map/psum | solution.py:23
  46.3 0.1 fusion.9
  46.5 4.9 %all-reduce = f32[192]{0:T(256)S(1)} all-reduce(f32[192]{0:T(256)S(1)} %bitcast.54), channel_id=2, replica_groups=mesh['gx'=4,'gy'=2,'gz'=4] {'gy'}, use_global_device_ids=true, to_apply=%region_2.0.clone | all-reduce | flops 192 | bytes 1536
  51.4 0.0 copy-done.2
  51.4 0.6 dynamic-slice
  52.7 0.1 dynamic-slice.1
  52.7 0.1 fusion.14
  52.8 1.3 fusion.3
  54.1 0.0 reduce-scatter.6.cloned.1.call-update
  54.2 0.0 reduce-scatter.8.cloned.1.call-start
  54.2 38.6 %reduce-scatter.10.cloned.1.call-done = f32[1,96,24]{1,2,0:T(8,128)} async-done(((f32[16,96,24]{1,2,0:T(8,128)}), f32[1,96,24]{1,2,0:T(8,128)}) %reduce-scatter.10.cloned.1.call-update) | async-done | bytes 9232
  92.8 0.7 convert_element_type.35
  93.6 1.4 fusion.1
  94.9 0.0 reduce-scatter.8.cloned.1.call-update
  94.9 64.0 %reduce-scatter.6.cloned.1.call-done = f32[1,6,2000]{2,1,0:T(8,128)} async-done(((f32[8,6,2000]{2,1,0:T(8,128)}), f32[1,6,2000]{2,1,0:T(8,128)}) %reduce-scatter.6.cloned.1.call-update) | async-done | bytes 48016 | tf_op jit(solution)/shard_map/reduce_scatter | solution.py:62
  159.0 65.6 %reduce-scatter.8.cloned.1.call-done = f32[1,6,2000]{2,1,0:T(8,128)} async-done(((f32[8,6,2000]{2,1,0:T(8,128)}), f32[1,6,2000]{2,1,0:T(8,128)}) %reduce-scatter.8.cloned.1.call-update) | async-done | bytes 48016 | tf_op jit(solution)/shard_map/reduce_scatter | solution.py:63
  (5 shorter events, 0.1 us)
Async XLA Ops:
  7.2 1.6 copy-start
  7.2 23.4 %slice-start = ((bf16[96,4000]{1,0:T(8,128)(2,1)}), bf16[96,96]{1,0:T(8,128)(2,1)S(1)}, s32[]{:S(2)}) async-start(bf16[96,4000]{1,0:T(8,128)(2,1)} %param.3), calls=%async_computation.6 | async-start | bytes 49152 | tf_op jit(solution)/shard_map/slice | solution.py:19
  7.2 23.5 %copy-start.1 = (bf16[192,1,384]{2,0,1:T(8,128)(2,1)S(1)}, bf16[192,1,384]{2,0,1:T(8,128)(2,1)}, u32[]{:S(2)}) copy-start(bf16[192,1,384]{2,0,1:T(8,128)(2,1)} %param.5) | copy-start | bytes 442372
  7.2 85.6 %reduce-scatter.10.cloned.1.call-start = ((), (), s32[]{:S(2)}) async-start(), calls=%async_computation.5 | async-start | bytes 208896
  30.7 20.7 %copy-start.2 = (u32[32]{0:T(128)S(1)}, u32[32]{0:T(128)}, u32[]{:S(2)}) copy-start(u32[32]{0:T(128)} %constant.15) | copy-start | bytes 388
  37.6 121.4 %reduce-scatter.6.cloned.1.call-start = ((), (), s32[]{:S(2)}) async-start(), calls=%async_computation.3 | async-start | bytes 589824 | tf_op jit(solution)/shard_map/reduce_scatter | solution.py:62
  54.2 170.5 %reduce-scatter.8.cloned.1.call-start = ((), (), s32[]{:S(2)}) async-start(), calls=%async_computation.4 | async-start | bytes 589824 | tf_op jit(solution)/shard_map/reduce_scatter | solution.py:63
Sparse Core Ops, SparseCore 0:
  37.7 55.0 reduce-scatter.9
  96.8 62.1 reduce-scatter.5
  162.9 61.6 reduce-scatter.7
where the time goes:
time: 231 us
  waiting for transfers between devices  168 us (73%)
  blocking collectives  36.1 us (16%)
  between operations  14.5 us (6%)
  local copies, waits for them, and re-layouts  5.63 us (2%)
  matrix products  5.53 us (2%)
    reduce_scatter x1, waiting for transfers between devices, local(): lax.psum_scatter(exch, ('gx', 'gy'), scatter_dimension=0, tiled=True)  65.6 us
    reduce_scatter x1, waiting for transfers between devices, local(): lax.psum_scatter(coul, ('gx', 'gy'), scatter_dimension=0, tiled=True)  64 us
    unnamed x4, waiting for transfers between devices  38.7 us
    all_gather x1, blocking collectives, local(): column_vals = lax.all_gather(occ_vals, 'gx', axis=0, tiled=True)  15.5 us
    psum x1, blocking collectives, local(): density = lax.psum(square_part, 'gz').astype(jnp.bfloat16)  5.67 us
    all_gather x1, blocking collectives, local(): win_piece = lax.all_gather(window_vals, 'gy', axis=0, tiled=True)  5.29 us
    unnamed x1, blocking collectives  4.93 us
    all_gather x1, blocking collectives, local(): occ_piece = lax.all_gather(occ_vals, 'gy', axis=0, tiled=True)  4.75 us
  transfers between devices with their start and end apart: 3, of which 3 were waited for; matrix products, arithmetic and copies ran while one was open for 3% of the time, Pallas kernels for 0%

commit v1 on v0

v1 whole, which is shorter than its diff:
```python
import functools

import jax
import jax.numpy as jnp
import numpy as np
from jax import lax
from jax.experimental import pallas as pl
from jax.experimental.pallas import tpu as pltpu
from jax.sharding import PartitionSpec as P

W = 96
LANES = 128
DEPTH = 1024
MESH = pl.DeviceIdType.MESH
F32 = jnp.float32
BF16 = jnp.bfloat16


def up(value, step):
    return -(-value // step) * step


def dot(left, right, left_dim, right_dim):
    return lax.dot_general(
        left, right, (((left_dim,), (right_dim,)), ((), ())), preferred_element_type=F32
    )


def kernel(
    dims,
    colloc_hbm,
    coeffs_hbm,
    core_hbm,
    place_hbm,
    coul_ref,
    exch_ref,
    vals,
    coeffs,
    core,
    place,
    col_occ,
    row_occ,
    wins,
    win_t,
    parts,
    pot_send,
    pot_recv,
    tot_send,
    tot_recv,
    y_send,
    y_recv,
    z_send,
    z_recv,
    load_sem,
    depth_sem,
    col_sem,
    row_sem,
    win_sem,
    pot_sem,
    tot_sem,
    y_sem,
    z_sem,
):
    gx_size, gy_size, gz_size, rows, pad_rows, width, piece = dims
    gx, gy, gz = lax.axis_index("gx"), lax.axis_index("gy"), lax.axis_index("gz")
    points, total = vals.shape
    band = gx_size * pad_rows
    pieces = parts.shape[1]

    def turn(pos, step, size):
        return lax.rem(pos + step, size) if step else pos

    def peer(dx, dy, dz):
        return (turn(gx, dx, gx_size), turn(gy, dy, gy_size), turn(gz, dz, gz_size))

    loads = [
        pltpu.make_async_copy(colloc_hbm, vals, load_sem.at[0]),
        pltpu.make_async_copy(core_hbm, core, load_sem.at[1]),
        pltpu.make_async_copy(place_hbm, place, load_sem.at[2]),
    ]
    spans = [(s, min(DEPTH, total - s)) for s in range(0, total, DEPTH)]
    depth_loads = [
        pltpu.make_async_copy(
            coeffs_hbm.at[pl.ds(s, n)], coeffs.at[pl.ds(s, n)], depth_sem.at[i]
        )
        for i, (s, n) in enumerate(spans)
    ]
    loads[0].start()
    for load in depth_loads:
        load.start()
    loads[1].start()
    loads[2].start()

    barrier = pltpu.get_barrier_semaphore()
    mates = [(dx, 0, dz) for dx in range(gx_size) for dz in range(gz_size) if dx or dz]
    mates += [(0, dy, dz) for dy in range(1, gy_size) for dz in range(gz_size)]
    for mate in mates:
        pl.semaphore_signal(barrier, inc=1, device_id=peer(*mate), device_id_type=MESH)

    sent = []

    def send(src, dst, sems, out_slot, in_slot, target):
        copy = pltpu.make_async_remote_copy(
            src_ref=src,
            dst_ref=dst,
            send_sem=sems.at[(0,) + out_slot],
            recv_sem=sems.at[(1,) + in_slot],
            device_id=target,
            device_id_type=MESH,
        )
        copy.start()
        sent.append(copy)

    def arrive(dst, sems, in_slot, source):
        pltpu.make_async_remote_copy(
            src_ref=dst,
            dst_ref=dst,
            send_sem=sems.at[(0,) + in_slot],
            recv_sem=sems.at[(1,) + in_slot],
            device_id=source,
            device_id_type=MESH,
        ).wait_recv()

    loads[0].wait()
    occ = jnp.zeros((points, coeffs.shape[1]), F32)
    for load, (s, n) in zip(depth_loads, spans):
        load.wait()
        occ += dot(vals[:, s : s + n], coeffs[s : s + n, :], 1, 0)
    occ = occ.astype(BF16)
    col_occ[gx] = occ
    row_occ[gy] = occ
    pl.semaphore_wait(barrier, len(mates))
    for dx in range(1, gx_size):
        send(col_occ.at[gx], col_occ.at[gx], col_sem, (dx,), (gx,), peer(dx, 0, 0))
    for dy in range(1, gy_size):
        send(row_occ.at[gy], row_occ.at[gy], row_sem, (dy,), (gy,), peer(0, dy, 0))
    window = vals.at[:, pl.ds(0, wins.shape[2])]
    for dy in range(1, gy_size):
        send(window, wins.at[gy], win_sem, (dy,), (gy,), peer(0, dy, 0))

    loads[1].wait()
    loads[2].wait()
    own_win = vals[:, : wins.shape[2]]
    wins[gy] = own_win
    spread = place[...]
    win_t[...] = dot(spread, own_win, 0, 1).reshape(gz_size, band, points)
    for h in range(gy_size):
        for c in range(pieces):
            s = h * width + c * piece
            n = min(piece, width - c * piece)
            parts[h, c, :, :n] = vals[:, s : s + n]
            if n < piece:
                parts[h, c, :, n:] = jnp.zeros((points, piece - n), BF16)

    for dy in range(1, gy_size):
        slot = turn(gy, dy, gy_size)
        arrive(wins.at[slot], win_sem, (slot,), peer(0, dy, 0))
    win_rows = dot(wins[...].reshape(gy_size * points, -1), spread, 1, 0).astype(BF16)
    for dx in range(1, gx_size):
        slot = turn(gx, dx, gx_size)
        arrive(col_occ.at[slot], col_sem, (slot,), peer(dx, 0, 0))
    cols = col_occ[...].reshape(gx_size * points, -1)
    square = jnp.square(cols.astype(F32))
    high = square.astype(BF16)
    low = (square - high.astype(F32)).astype(BF16)
    ones = jnp.ones((8, square.shape[1]), BF16)
    density = dot(ones, high, 1, 1) + dot(ones, low, 1, 1)
    core_vals = core[...]
    potential = dot(density.astype(BF16), core_vals, 1, 1)
    for h in range(gy_size):
        pot_send[h] = potential[:, h * points : (h + 1) * points]
    mine = gy * gz_size + gz
    for dy in range(gy_size):
        for dz in range(gz_size):
            if dy or dz:
                src = pot_send.at[turn(gy, dy, gy_size)]
                out = (dy * gz_size + dz,)
                send(src, pot_recv.at[mine], pot_sem, out, (mine,), peer(0, dy, dz))

    for dy in range(1, gy_size):
        slot = turn(gy, dy, gy_size)
        arrive(row_occ.at[slot], row_sem, (slot,), peer(0, dy, 0))
    gram = dot(row_occ[...].reshape(gy_size * points, -1), cols, 1, 1)
    mixed = (core_vals.astype(F32) * gram).astype(BF16)
    totals = dot(win_rows, mixed, 0, 0)
    for a in range(gx_size):
        block = totals[:, a * points : (a + 1) * points].astype(BF16)
        tot_send[a] = block.reshape(gz_size, band, points)
    home = gx * gz_size + gz
    for dx in range(gx_size):
        for dz in range(gz_size):
            if dx or dz:
                to = peer(dx, 0, dz)
                src = tot_send.at[to[0], to[2]]
                out = (dx * gz_size + dz,)
                send(src, tot_recv.at[home], tot_sem, out, (home,), to)

    def spread_out(index, left):
        kept = []
        for c in range(pieces):
            for dy in range(1, gy_size):
                h = turn(gy, dy, gy_size)
                y_send[index, c, h] = dot(left, parts[h, c], 1, 0).astype(BF16)
                slots = (index, c, dy), (index, c, gy)
                dst = y_recv.at[index, c, gy]
                send(y_send.at[index, c, h], dst, y_sem, *slots, peer(0, dy, 0))
        for c in range(pieces):
            kept.append(dot(left, parts[gy, c], 1, 0))
        return kept

    pot = pot_send[gy]
    for dy in range(gy_size):
        for dz in range(gz_size):
            if dy or dz:
                to = peer(0, dy, dz)
                slot = to[1] * gz_size + to[2]
                arrive(pot_recv.at[slot], pot_sem, (slot,), to)
                pot += pot_recv[slot]
    coul_kept = spread_out(0, (win_t[gz] * pot[:1]).astype(BF16))

    owned = tot_send[gx, gz].astype(F32)
    for dx in range(gx_size):
        for dz in range(gz_size):
            if dx or dz:
                to = peer(dx, 0, dz)
                slot = to[0] * gz_size + to[2]
                arrive(tot_recv.at[slot], tot_sem, (slot,), to)
                owned += tot_recv[slot].astype(F32)
    exch_kept = spread_out(1, owned.astype(BF16))

    for index, kept in enumerate((coul_kept, exch_kept)):
        for c in range(pieces):
            acc = kept[c]
            for dy in range(1, gy_size):
                slot = turn(gy, dy, gy_size)
                dst = y_recv.at[index, c, slot]
                arrive(dst, y_sem, (index, c, slot), peer(0, dy, 0))
                acc += y_recv[index, c, slot].astype(F32)
            z_send[index, c] = acc.reshape(gx_size, pad_rows, piece).astype(BF16)
            for dx in range(1, gx_size):
                a = turn(gx, dx, gx_size)
                slots = (index, c, dx), (index, c, gx)
                dst = z_recv.at[index, c, gx]
                send(z_send.at[index, c, a], dst, z_sem, *slots, peer(dx, 0, 0))

    for index, out_ref in enumerate((coul_ref, exch_ref)):
        for c in range(pieces):
            acc = z_send[index, c, gx].astype(F32)
            for dx in range(1, gx_size):
                slot = turn(gx, dx, gx_size)
                dst = z_recv.at[index, c, slot]
                arrive(dst, z_sem, (index, c, slot), peer(dx, 0, 0))
                acc += z_recv[index, c, slot].astype(F32)
            n = min(piece, width - c * piece)
            out_ref[:, c * piece : c * piece + n] = acc[:rows, :n]

    for copy in sent:
        copy.wait_send()


def local(colloc, occ_coeffs, core):
    points, total = colloc.shape
    gx_size = lax.axis_size("gx")
    gy_size = lax.axis_size("gy")
    gz_size = lax.axis_size("gz")
    occupied = occ_coeffs.shape[1]
    rows = W // (gx_size * gz_size)
    pad_rows = up(rows, 8)
    width = total // gy_size
    piece = min(512, up(width, LANES))
    pieces = -(-width // piece)
    row_count, flat = core.shape[0], core.shape[2]
    band = gx_size * pad_rows
    lanes = up(W, LANES)

    place = np.zeros((lanes, gz_size, gx_size, pad_rows), np.float32)
    for a in range(gx_size):
        for g in range(gz_size):
            for k in range(rows):
                place[(a * gz_size + g) * rows + k, g, a, k] = 1
    place = jnp.asarray(place.reshape(lanes, gz_size * band), BF16)

    dims = (gx_size, gy_size, gz_size, rows, pad_rows, width, piece)
    dma = pltpu.SemaphoreType.DMA
    vmem = pltpu.VMEM
    out = jax.ShapeDtypeStruct((rows, width), F32)
    return pl.pallas_call(
        functools.partial(kernel, dims),
        out_shape=(out, out),
        in_specs=[pl.BlockSpec(memory_space=pltpu.HBM)] * 4,
        out_specs=(pl.BlockSpec(memory_space=pltpu.VMEM),) * 2,
        scratch_shapes=[
            vmem((points, total), BF16),
            vmem((total, occupied), BF16),
            vmem((row_count, flat), BF16),
            vmem((lanes, gz_size * band), BF16),
            vmem((gx_size, points, occupied), BF16),
            vmem((gy_size, points, occupied), BF16),
            vmem((gy_size, points, lanes), BF16),
            vmem((gz_size, band, points), F32),
            vmem((gy_size, pieces, points, piece), BF16),
            vmem((gy_size, 8, points), F32),
            vmem((gy_size * gz_size, 8, points), F32),
            vmem((gx_size, gz_size, band, points), BF16),
            vmem((gx_size * gz_size, band, points), BF16),
            vmem((2, pieces, gy_size, band, piece), BF16),
            vmem((2, pieces, gy_size, band, piece), BF16),
            vmem((2, pieces, gx_size, pad_rows, piece), BF16),
            vmem((2, pieces, gx_size, pad_rows, piece), BF16),
            dma((3,)),
            dma((-(-total // DEPTH),)),
            dma((2, gx_size)),
            dma((2, gy_size)),
            dma((2, gy_size)),
            dma((2, gy_size * gz_size)),
            dma((2, gx_size * gz_size)),
            dma((2, 2, pieces, gy_size)),
            dma((2, 2, pieces, gx_size)),
        ],
        compiler_params=pltpu.CompilerParams(
            collective_id=0, has_side_effects=True, vmem_limit_bytes=48 * 1024 * 1024
        ),
    )(colloc, occ_coeffs, core.reshape(row_count, flat), place)


def solution(mesh):
    in_specs = (P(("gx", "gy"), None), P(None, "gz"), P("gx", "gy", None))
    out_specs = (P(("gx", "gz"), "gy"), P(("gx", "gz"), "gy"))
    return jax.shard_map(local, mesh=mesh, in_specs=in_specs, out_specs=out_specs, check_vma=False)
```

time: 231 us -> 36.1 us (0.16)
  waiting for transfers between devices: 168 us -> 0 us
  blocking collectives: 36.1 us -> 0 us
  Pallas kernels: 0 us -> 29.5 us
  between operations: 14.5 us -> 0.65 us
  matrix products: 5.53 us -> 0 us
    reduce_scatter x2 -> x0, waiting for transfers between devices: 130 us -> none  [the longest x1 65.6 us: local(): lax.psum_scatter(exch, ('gx', 'gy'), scatter_dimension=0, tiled=True)]
    unnamed x4 -> x0, waiting for transfers between devices: 38.7 us -> none
    pallas_call x0 -> x1, Pallas kernels: none -> 29.5 us  [local(): pl.pallas_call(functools.partial(kernel, dims), out_shape=(out, out), in_...]
    all_gather x3 -> x0, blocking collectives: 25.5 us -> none  [the longest x1 15.5 us: local(): column_vals = lax.all_gather(occ_vals, 'gx', axis=0, tiled=True)]
    psum x1 -> x0, blocking collectives: 5.67 us -> none  [local(): density = lax.psum(square_part, 'gz').astype(jnp.bfloat16)]
    dot_general x6 -> x0, matrix products: 5.53 us -> none  [the longest x1 1.59 us: local(): jnp.dot(colloc, occ_coeffs, preferred_element_type=jnp.float32)]
    unnamed x1 -> x0, blocking collectives: 4.93 us -> none
    unnamed x8 -> x10, local copies, waits for them, and re-layouts: 2.17 us -> 5.63 us
  transfers between devices with their start and end apart: 3 -> 0, of which waited for: 3 -> 0; matrix products, arithmetic and copies ran while one was open for 3% -> 0% of each run, Pallas kernels for 0% -> 0%
where the time goes in v1:
time: 36.1 us; the launch traced here: 35.8 us
  Pallas kernels  29.5 us (82%)
  local copies, waits for them, and re-layouts  5.63 us (16%)
  between operations  0.65 us (2%)
    pallas_call x1, Pallas kernels, local(): pl.pallas_call(functools.partial(kernel, dims), out_shape=(out, out), in_...  29.5 us
    unnamed x10, local copies, waits for them, and re-layouts  5.63 us

profile of v1, /device:TPU:0, one launch (start us, length us, event | category | flops | bytes accessed | tf_op | source)
XLA Modules:
  0.0 35.8 jit_solution(12585705926022216829)
XLA Ops:
  0.6 0.0 copy-start
  0.6 1.6 %copy-done = bf16[4000,256]{1,0:T(8,128)(2,1)S(1)} copy-done((bf16[4000,256]{1,0:T(8,128)(2,1)S(1)}, bf16[4000,256]{1,0:T(8,128)(2,1)}, u32[]{:S(2)}) %copy-start) | copy-done | bytes 2048024
  2.2 0.0 copy-start.1
  2.2 1.1 %copy-done.1 = bf16[96,4000]{1,0:T(8,128)(2,1)S(1)} copy-done((bf16[96,4000]{1,0:T(8,128)(2,1)S(1)}, bf16[96,4000]{1,0:T(8,128)(2,1)}, u32[]{:S(2)}) %copy-start.1) | copy-done | bytes 768024
  3.3 0.0 copy-start.2
  3.3 0.9 %copy-done.2 = bf16[192,1,384]{2,0,1:T(8,128)(2,1)S(1)} copy-done((bf16[192,1,384]{2,0,1:T(8,128)(2,1)S(1)}, bf16[192,1,384]{2,0,1:T(8,128)(2,1)}, u32[]{:S(2)}) %copy-start.2) | copy-done | bytes 147480
  4.2 0.0 copy-start.3
  4.3 0.8 %copy-done.3 = bf16[128,128]{1,0:T(8,128)(2,1)S(1)} copy-done((bf16[128,128]{1,0:T(8,128)(2,1)S(1)}, bf16[128,128]{1,0:T(8,128)(2,1)}, u32[]{:S(2)}) %copy-start.3) | copy-done | bytes 32792
  5.0 29.5 %shard_map.59 = (f32[6,2000]{1,0:T(8,128)S(1)}, f32[6,2000]{1,0:T(8,128)S(1)}) custom-call(bf16[96,4000]{1,0:T(8,128)(2,1)S(1)} %copy-done.1, bf16[4000,256]{1,0:T(8,128)(2,1)S(1)} %copy-done, bf16[192,384]{1,0:T(8,128)(2,1)S(1)} %bitcast.1, bf16[128,128]{1,0:T(8,128)(2,1)S(1)} %copy-done.3), custom_call_target="tpu_custom_call" | custom-call | tf_op jit(solution)/shard_map/pallas_call | solution.py:287
  34.5 0.6 %copy.8 = f32[6,2000]{1,0:T(8,128)} copy(f32[6,2000]{1,0:T(8,128)S(1)} %get-tuple-element.4) | data formatting | bytes 96000
  35.2 0.6 %copy.9 = f32[6,2000]{1,0:T(8,128)} copy(f32[6,2000]{1,0:T(8,128)S(1)} %get-tuple-element.5) | data formatting | bytes 96000
Async XLA Ops:
  0.6 1.6 %copy-start = (bf16[4000,256]{1,0:T(8,128)(2,1)S(1)}, bf16[4000,256]{1,0:T(8,128)(2,1)}, u32[]{:S(2)}) copy-start(bf16[4000,256]{1,0:T(8,128)(2,1)} %coeffs_hbm.1) | copy-start | bytes 6144004
  2.2 1.1 %copy-start.1 = (bf16[96,4000]{1,0:T(8,128)(2,1)S(1)}, bf16[96,4000]{1,0:T(8,128)(2,1)}, u32[]{:S(2)}) copy-start(bf16[96,4000]{1,0:T(8,128)(2,1)} %colloc_hbm.1) | copy-start | bytes 2304004
  3.3 0.9 %copy-start.2 = (bf16[192,1,384]{2,0,1:T(8,128)(2,1)S(1)}, bf16[192,1,384]{2,0,1:T(8,128)(2,1)}, u32[]{:S(2)}) copy-start(bf16[192,1,384]{2,0,1:T(8,128)(2,1)} %param.6) | copy-start | bytes 442372
  4.2 0.8 %copy-start.3 = (bf16[128,128]{1,0:T(8,128)(2,1)S(1)}, bf16[128,128]{1,0:T(8,128)(2,1)}, u32[]{:S(2)}) copy-start(bf16[128,128]{1,0:T(8,128)(2,1)} %constant.2.clone.place_hbm) | copy-start | bytes 98308

commit v2 on v1

--- a/solution.py
+++ b/solution.py
@@ -32,12 +32,14 @@
     coeffs_hbm,
     core_hbm,
     place_hbm,
-    coul_ref,
-    exch_ref,
+    fold_hbm,
+    out_ref,
     vals,
     coeffs,
     core,
     place,
+    fold,
+    cores,
     col_occ,
     row_occ,
     wins,
@@ -61,14 +63,21 @@
     y_sem,
     z_sem,
 ):
-    gx_size, gy_size, gz_size, rows, pad_rows, width, piece = dims
+    gx_size, gy_size, gz_size, rows, pad_rows, width, piece, tails = dims
     gx, gy, gz = lax.axis_index("gx"), lax.axis_index("gy"), lax.axis_index("gz")
     points, total = vals.shape
     band = gx_size * pad_rows
     pieces = parts.shape[1]
 
     def turn(pos, step, size):
-        return lax.rem(pos + step, size) if step else pos
+        if size & (size - 1):
+            return lax.rem(pos + step, size) if step else pos
+        bit = 1
+        while bit <= step:
+            if step & bit:
+                pos = pos + bit * (1 - 2 * lax.rem(lax.div(pos, bit), 2))
+            bit *= 2
+        return pos
 
     def peer(dx, dy, dz):
         return (turn(gx, dx, gx_size), turn(gy, dy, gy_size), turn(gz, dz, gz_size))
@@ -77,6 +86,7 @@
         pltpu.make_async_copy(colloc_hbm, vals, load_sem.at[0]),
         pltpu.make_async_copy(core_hbm, core, load_sem.at[1]),
         pltpu.make_async_copy(place_hbm, place, load_sem.at[2]),
+        pltpu.make_async_copy(fold_hbm, fold, load_sem.at[3]),
     ]
     spans = [(s, min(DEPTH, total - s)) for s in range(0, total, DEPTH)]
     depth_loads = [
@@ -90,6 +100,7 @@
         load.start()
     loads[1].start()
     loads[2].start()
+    loads[3].start()
 
     barrier = pltpu.get_barrier_semaphore()
     mates = [(dx, 0, dz) for dx in range(gx_size) for dz in range(gz_size) if dx or dz]
@@ -122,51 +133,79 @@
         ).wait_recv()
 
     loads[0].wait()
+    window = vals.at[:, pl.ds(0, wins.shape[2])]
     occ = jnp.zeros((points, coeffs.shape[1]), F32)
     for load, (s, n) in zip(depth_loads, spans):
         load.wait()
+        if s == spans[-1][0]:
+            pl.semaphore_wait(barrier, len(mates))
+            for dy in range(1, gy_size):
+                send(window, wins.at[gy], win_sem, (dy,), (gy,), peer(0, dy, 0))
         occ += dot(vals[:, s : s + n], coeffs[s : s + n, :], 1, 0)
     occ = occ.astype(BF16)
     col_occ[gx] = occ
     row_occ[gy] = occ
-    pl.semaphore_wait(barrier, len(mates))
-    for dx in range(1, gx_size):
-        send(col_occ.at[gx], col_occ.at[gx], col_sem, (dx,), (gx,), peer(dx, 0, 0))
     for dy in range(1, gy_size):
         send(row_occ.at[gy], row_occ.at[gy], row_sem, (dy,), (gy,), peer(0, dy, 0))
-    window = vals.at[:, pl.ds(0, wins.shape[2])]
-    for dy in range(1, gy_size):
-        send(window, wins.at[gy], win_sem, (dy,), (gy,), peer(0, dy, 0))
-
-    loads[1].wait()
-    loads[2].wait()
+    for dx in reversed(range(1, gx_size)):
+        send(col_occ.at[gx], col_occ.at[gx], col_sem, (dx,), (gx,), peer(dx, 0, 0))
+
+    for load in loads[1:]:
+        load.wait()
     own_win = vals[:, : wins.shape[2]]
     wins[gy] = own_win
     spread = place[...]
     win_t[...] = dot(spread, own_win, 0, 1).reshape(gz_size, band, points)
+    for a in range(gx_size):
+        cores[a] = core[:, a * points : (a + 1) * points]
+
+    def fill(h, c, u, unit):
+        at = pl.ds(u * points, points)
+        n = min(piece, width - unit * piece)
+        s = h * width + unit * piece
+        parts[h, c, at, :n] = vals[:, s : s + n]
+        if n < piece:
+            parts[h, c, at, n:] = jnp.zeros((points, piece - n), BF16)
+
     for h in range(gy_size):
         for c in range(pieces):
-            s = h * width + c * piece
-            n = min(piece, width - c * piece)
-            parts[h, c, :, :n] = vals[:, s : s + n]
-            if n < piece:
-                parts[h, c, :, n:] = jnp.zeros((points, piece - n), BF16)
+            fill(h, c, 0, c)
+            for u in range(tails):
+                fill(h, c, 1 + u, pieces + u)
 
     for dy in range(1, gy_size):
         slot = turn(gy, dy, gy_size)
         arrive(wins.at[slot], win_sem, (slot,), peer(0, dy, 0))
-    win_rows = dot(wins[...].reshape(gy_size * points, -1), spread, 1, 0).astype(BF16)
-    for dx in range(1, gx_size):
-        slot = turn(gx, dx, gx_size)
-        arrive(col_occ.at[slot], col_sem, (slot,), peer(dx, 0, 0))
-    cols = col_occ[...].reshape(gx_size * points, -1)
-    square = jnp.square(cols.astype(F32))
-    high = square.astype(BF16)
-    low = (square - high.astype(F32)).astype(BF16)
-    ones = jnp.ones((8, square.shape[1]), BF16)
-    density = dot(ones, high, 1, 1) + dot(ones, low, 1, 1)
-    core_vals = core[...]
-    potential = dot(density.astype(BF16), core_vals, 1, 1)
+    win_rows = dot(spread, wins[...].reshape(gy_size * points, -1), 0, 1).astype(BF16)
+    for dy in range(1, gy_size):
+        slot = turn(gy, dy, gy_size)
+        arrive(row_occ.at[slot], row_sem, (slot,), peer(0, dy, 0))
+    row_vals = row_occ[...].reshape(gy_size * points, -1)
+
+    home = gx * gz_size + gz
+    ones = jnp.ones((8, coeffs.shape[1]), BF16)
+    potential = jnp.zeros((8, gy_size * points), F32)
+    for dx in range(gx_size):
+        a = turn(gx, dx, gx_size)
+        if dx:
+            arrive(col_occ.at[a], col_sem, (a,), peer(dx, 0, 0))
+        cols = col_occ[a]
+        core_vals = cores[a]
+        gram = dot(row_vals, cols, 1, 1)
+        mixed = (core_vals.astype(F32) * gram).astype(BF16)
+        block = dot(win_rows, mixed, 1, 0).astype(BF16)
+        tot_send[a] = block.reshape(gz_size, band, points)
+        for dz in range(gz_size):
+            if dx or dz:
+                to = peer(dx, 0, dz)
+                src = tot_send.at[a, to[2]]
+                out = (dx * gz_size + dz,)
+                send(src, tot_recv.at[home], tot_sem, out, (home,), to)
+        square = jnp.square(cols.astype(F32))
+        high = square.astype(BF16)
+        low = (square - high.astype(F32)).astype(BF16)
+        density = dot(ones, high, 1, 1) + dot(ones, low, 1, 1)
+        potential += dot(density.astype(BF16), core_vals, 1, 1)
     for h in range(gy_size):
         pot_send[h] = potential[:, h * points : (h + 1) * points]
     mine = gy * gz_size + gz
@@ -177,35 +216,25 @@
                 out = (dy * gz_size + dz,)
                 send(src, pot_recv.at[mine], pot_sem, out, (mine,), peer(0, dy, dz))
 
-    for dy in range(1, gy_size):
-        slot = turn(gy, dy, gy_size)
-        arrive(row_occ.at[slot], row_sem, (slot,), peer(0, dy, 0))
-    gram = dot(row_occ[...].reshape(gy_size * points, -1), cols, 1, 1)
-    mixed = (core_vals.astype(F32) * gram).astype(BF16)
-    totals = dot(win_rows, mixed, 0, 0)
-    for a in range(gx_size):
-        block = totals[:, a * points : (a + 1) * points].astype(BF16)
-        tot_send[a] = block.reshape(gz_size, band, points)
-    home = gx * gz_size + gz
-    for dx in range(gx_size):
-        for dz in range(gz_size):
-            if dx or dz:
-                to = peer(dx, 0, dz)
-                src = tot_send.at[to[0], to[2]]
-                out = (dx * gz_size + dz,)
-                send(src, tot_recv.at[home], tot_sem, out, (home,), to)
-
     def spread_out(index, left):
         kept = []
+        lefts = [left] * pieces
+        if tails:
+            folded = dot(fold[...], left, 1, 0).astype(BF16)
+            folded = folded.reshape(pieces, tails, band, points)
+            lefts = [
+                jnp.concatenate([left] + [folded[c, u] for u in range(tails)], axis=1)
+                for c in range(pieces)
+            ]
         for c in range(pieces):
             for dy in range(1, gy_size):
                 h = turn(gy, dy, gy_size)
-                y_send[index, c, h] = dot(left, parts[h, c], 1, 0).astype(BF16)
+                y_send[index, c, h] = dot(lefts[c], parts[h, c], 1, 0).astype(BF16)
                 slots = (index, c, dy), (index, c, gy)
                 dst = y_recv.at[index, c, gy]
                 send(y_send.at[index, c, h], dst, y_sem, *slots, peer(0, dy, 0))
         for c in range(pieces):
-            kept.append(dot(left, parts[gy, c], 1, 0))
+            kept.append(dot(lefts[c], parts[gy, c], 1, 0))
         return kept
 
     pot = pot_send[gy]
@@ -243,7 +272,8 @@
                 dst = z_recv.at[index, c, gx]
                 send(z_send.at[index, c, a], dst, z_sem, *slots, peer(dx, 0, 0))
 
-    for index, out_ref in enumerate((coul_ref, exch_ref)):
+    spare = pad_rows - rows
+    for index in range(2):
         for c in range(pieces):
             acc = z_send[index, c, gx].astype(F32)
             for dx in range(1, gx_size):
@@ -252,7 +282,14 @@
                 arrive(dst, z_sem, (index, c, slot), peer(dx, 0, 0))
                 acc += z_recv[index, c, slot].astype(F32)
             n = min(piece, width - c * piece)
-            out_ref[:, c * piece : c * piece + n] = acc[:rows, :n]
+            out_ref[index, :, c * piece : c * piece + n] = acc[:rows, :n]
+            for s in range(spare):
+                u, r = divmod(c * spare + s, rows)
+                if u < tails:
+                    start = (pieces + u) * piece
+                    n = min(piece, width - start)
+                    line = acc[rows + s : rows + s + 1, :n]
+                    out_ref[index, r : r + 1, start : start + n] = line
 
     for copy in sent:
         copy.wait_send()
@@ -267,8 +304,11 @@
     rows = W // (gx_size * gz_size)
     pad_rows = up(rows, 8)
     width = total // gy_size
-    piece = min(512, up(width, LANES))
-    pieces = -(-width // piece)
+    piece = 512 if width > 512 else LANES
+    units = -(-width // piece)
+    spare = pad_rows - rows
+    pieces = next(q for q in range(1, units + 1) if (units - q) * rows <= q * spare)
+    tails = units - pieces
     row_count, flat = core.shape[0], core.shape[2]
     band = gx_size * pad_rows
     lanes = up(W, LANES)
@@ -280,25 +320,35 @@
                 place[(a * gz_size + g) * rows + k, g, a, k] = 1
     place = jnp.asarray(place.reshape(lanes, gz_size * band), BF16)
 
-    dims = (gx_size, gy_size, gz_size, rows, pad_rows, width, piece)
+    fold = np.zeros((pieces, max(tails, 1), band, band), np.float32)
+    for c in range(pieces):
+        for s in range(spare):
+            u, r = divmod(c * spare + s, rows)
+            if u < tails:
+                for a in range(0, band, pad_rows):
+                    fold[c, u, a + rows + s, a + r] = 1
+    fold = jnp.asarray(fold.reshape(-1, band), BF16)
+
+    dims = (gx_size, gy_size, gz_size, rows, pad_rows, width, piece, tails)
     dma = pltpu.SemaphoreType.DMA
     vmem = pltpu.VMEM
-    out = jax.ShapeDtypeStruct((rows, width), F32)
-    return pl.pallas_call(
+    result = pl.pallas_call(
         functools.partial(kernel, dims),
-        out_shape=(out, out),
-        in_specs=[pl.BlockSpec(memory_space=pltpu.HBM)] * 4,
-        out_specs=(pl.BlockSpec(memory_space=pltpu.VMEM),) * 2,
+        out_shape=jax.ShapeDtypeStruct((2, rows, width), F32),
+        in_specs=[pl.BlockSpec(memory_space=pltpu.HBM)] * 5,
+        out_specs=pl.BlockSpec(memory_space=pltpu.VMEM),
         scratch_shapes=[
             vmem((points, total), BF16),
             vmem((total, occupied), BF16),
             vmem((row_count, flat), BF16),
             vmem((lanes, gz_size * band), BF16),
+            vmem(fold.shape, BF16),
+            vmem((gx_size, row_count, points), BF16),
             vmem((gx_size, points, occupied), BF16),
             vmem((gy_size, points, occupied), BF16),
             vmem((gy_size, points, lanes), BF16),
             vmem((gz_size, band, points), F32),
-            vmem((gy_size, pieces, points, piece), BF16),
+            vmem((gy_size, pieces, (1 + tails) * points, piece), BF16),
             vmem((gy_size, 8, points), F32),
             vmem((gy_size * gz_size, 8, points), F32),
             vmem((gx_size, gz_size, band, points), BF16),
@@ -307,7 +357,7 @@
             vmem((2, pieces, gy_size, band, piece), BF16),
             vmem((2, pieces, gx_size, pad_rows, piece), BF16),
             vmem((2, pieces, gx_size, pad_rows, piece), BF16),
-            dma((3,)),
+            dma((4,)),
             dma((-(-total // DEPTH),)),
             dma((2, gx_size)),
             dma((2, gy_size)),
@@ -318,9 +368,10 @@
             dma((2, 2, pieces, gx_size)),
         ],
         compiler_params=pltpu.CompilerParams(
-            collective_id=0, has_side_effects=True, vmem_limit_bytes=48 * 1024 * 1024
+            collective_id=0, has_side_effects=True, vmem_limit_bytes=67043328
         ),
-    )(colloc, occ_coeffs, core.reshape(row_count, flat), place)
+    )(colloc, occ_coeffs, core.reshape(row_count, flat), place, fold)
+    return result[0], result[1]
 
 
 def solution(mesh):

time: 36.1 us -> 31.1 us (0.86)
  local copies, waits for them, and re-layouts: 5.63 us -> 1.53 us
  Pallas kernels: 29.5 us -> 28.7 us
    unnamed x10 -> x0, local copies, waits for them, and re-layouts: 5.63 us -> none
    squeeze x0 -> x1, local copies, waits for them, and re-layouts: none -> 1.53 us  [local(): return (result[0], result[1])]
    pallas_call x1, Pallas kernels: 29.5 us -> 28.7 us  [local(): pl.pallas_call(functools.partial(kernel, dims), out_shape=jax.ShapeDtypeS...]
where the time goes in v2:
time: 31.1 us; the launch traced here: 30.9 us
  Pallas kernels  28.7 us (92%)
  local copies, waits for them, and re-layouts  1.53 us (5%)
  between operations  0.64 us (2%)
    pallas_call x1, Pallas kernels, local(): pl.pallas_call(functools.partial(kernel, dims), out_shape=jax.ShapeDtypeS...  28.7 us
    squeeze x1, local copies, waits for them, and re-layouts, local(): return (result[0], result[1])  1.53 us

profile of v2, /device:TPU:0, one launch (start us, length us, event | category | flops | bytes accessed | tf_op | source)
XLA Modules:
  0.0 30.9 jit_solution(12591396394083698585)
XLA Ops:
  0.6 28.7 %shard_map.68 = f32[2,6,2000]{2,1,0:T(8,128)} custom-call(bf16[96,4000]{1,0:T(8,128)(2,1)} %colloc_hbm.1, bf16[4000,256]{1,0:T(8,128)(2,1)} %coeffs_hbm.1, bf16[192,384]{1,0:T(8,128)(2,1)} %bitcast.5, bf16[128,128]{1,0:T(8,128)(2,1)} %constant.4.clone.place_hbm, bf16[96,32]{1,0:T(8,128)(2,1)} %constant.5.clone.fold_hbm), custom_call_target="tpu_custom_call" | custom-call | tf_op jit(solution)/shard_map/pallas_call | solution.py:335
  29.4 1.5 %slice_bitcast_fusion = (f32[6,2000]{1,0:T(8,128)}, f32[6,2000]{1,0:T(8,128)}) fusion(f32[2,6,2000]{2,1,0:T(8,128)} %shard_map.68), kind=kLoop, calls=%fused_computation | loop fusion | bytes 192000 | tf_op jit(solution)/shard_map/squeeze | solution.py:374

commit v3 on v2

--- a/solution.py
+++ b/solution.py
@@ -68,6 +68,7 @@
     points, total = vals.shape
     band = gx_size * pad_rows
     pieces = parts.shape[1]
+    slabs, _, slab = coeffs.shape
 
     def turn(pos, step, size):
         if size & (size - 1):
@@ -91,8 +92,11 @@
     spans = [(s, min(DEPTH, total - s)) for s in range(0, total, DEPTH)]
     depth_loads = [
         pltpu.make_async_copy(
-            coeffs_hbm.at[pl.ds(s, n)], coeffs.at[pl.ds(s, n)], depth_sem.at[i]
+            coeffs_hbm.at[pl.ds(s, n), pl.ds(q * slab, slab)],
+            coeffs.at[q, pl.ds(s, n)],
+            depth_sem.at[q, i],
         )
+        for q in range(slabs)
         for i, (s, n) in enumerate(spans)
     ]
     loads[0].start()
@@ -134,21 +138,27 @@
 
     loads[0].wait()
     window = vals.at[:, pl.ds(0, wins.shape[2])]
-    occ = jnp.zeros((points, coeffs.shape[1]), F32)
-    for load, (s, n) in zip(depth_loads, spans):
-        load.wait()
-        if s == spans[-1][0]:
+    for q in range(slabs):
+        occ = jnp.zeros((points, slab), F32)
+        for i, (s, n) in enumerate(spans):
+            depth_loads[q * len(spans) + i].wait()
+            occ += dot(vals[:, s : s + n], coeffs[q, s : s + n, :], 1, 0)
+        occ = occ.astype(BF16)
+        col_occ[gx, q] = occ
+        row_occ[gy, q] = occ
+        if q == 0:
             pl.semaphore_wait(barrier, len(mates))
+        for dx in reversed(range(1, gx_size)):
+            slots = (dx, q), (gx, q)
+            src = col_occ.at[gx, q]
+            send(src, src, col_sem, *slots, peer(dx, 0, 0))
+        for dy in range(1, gy_size):
+            slots = (dy, q), (gy, q)
+            src = row_occ.at[gy, q]
+            send(src, src, row_sem, *slots, peer(0, dy, 0))
+        if q == 0:
             for dy in range(1, gy_size):
                 send(window, wins.at[gy], win_sem, (dy,), (gy,), peer(0, dy, 0))
-        occ += dot(vals[:, s : s + n], coeffs[s : s + n, :], 1, 0)
-    occ = occ.astype(BF16)
-    col_occ[gx] = occ
-    row_occ[gy] = occ
-    for dy in range(1, gy_size):
-        send(row_occ.at[gy], row_occ.at[gy], row_sem, (dy,), (gy,), peer(0, dy, 0))
-    for dx in reversed(range(1, gx_size)):
-        send(col_occ.at[gx], col_occ.at[gx], col_sem, (dx,), (gx,), peer(dx, 0, 0))
 
     for load in loads[1:]:
         load.wait()
@@ -179,17 +189,20 @@
     win_rows = dot(spread, wins[...].reshape(gy_size * points, -1), 0, 1).astype(BF16)
     for dy in range(1, gy_size):
         slot = turn(gy, dy, gy_size)
-        arrive(row_occ.at[slot], row_sem, (slot,), peer(0, dy, 0))
-    row_vals = row_occ[...].reshape(gy_size * points, -1)
+        for q in range(slabs):
+            arrive(row_occ.at[slot, q], row_sem, (slot, q), peer(0, dy, 0))
+    row_vals = [row_occ[:, q].reshape(gy_size * points, slab) for q in range(slabs)]
+    row_vals = jnp.concatenate(row_vals, axis=1)
 
     home = gx * gz_size + gz
-    ones = jnp.ones((8, coeffs.shape[1]), BF16)
+    ones = jnp.ones((8, slabs * slab), BF16)
     potential = jnp.zeros((8, gy_size * points), F32)
     for dx in range(gx_size):
         a = turn(gx, dx, gx_size)
         if dx:
-            arrive(col_occ.at[a], col_sem, (a,), peer(dx, 0, 0))
-        cols = col_occ[a]
+            for q in range(slabs):
+                arrive(col_occ.at[a, q], col_sem, (a, q), peer(dx, 0, 0))
+        cols = jnp.concatenate([col_occ[a, q] for q in range(slabs)], axis=1)
         core_vals = cores[a]
         gram = dot(row_vals, cols, 1, 1)
         mixed = (core_vals.astype(F32) * gram).astype(BF16)
@@ -310,6 +323,8 @@
     pieces = next(q for q in range(1, units + 1) if (units - q) * rows <= q * spare)
     tails = units - pieces
     row_count, flat = core.shape[0], core.shape[2]
+    slab = LANES if occupied % LANES == 0 else occupied
+    slabs = occupied // slab
     band = gx_size * pad_rows
     lanes = up(W, LANES)
 
@@ -334,18 +349,18 @@
     vmem = pltpu.VMEM
     result = pl.pallas_call(
         functools.partial(kernel, dims),
-        out_shape=jax.ShapeDtypeStruct((2, rows, width), F32),
+        out_shape=pltpu.VMEM((2, rows, width), F32),
         in_specs=[pl.BlockSpec(memory_space=pltpu.HBM)] * 5,
         out_specs=pl.BlockSpec(memory_space=pltpu.VMEM),
         scratch_shapes=[
             vmem((points, total), BF16),
-            vmem((total, occupied), BF16),
+            vmem((slabs, total, slab), BF16),
             vmem((row_count, flat), BF16),
             vmem((lanes, gz_size * band), BF16),
             vmem(fold.shape, BF16),
             vmem((gx_size, row_count, points), BF16),
-            vmem((gx_size, points, occupied), BF16),
-            vmem((gy_size, points, occupied), BF16),
+            vmem((gx_size, slabs, points, slab), BF16),
+            vmem((gy_size, slabs, points, slab), BF16),
             vmem((gy_size, points, lanes), BF16),
             vmem((gz_size, band, points), F32),
             vmem((gy_size, pieces, (1 + tails) * points, piece), BF16),
@@ -358,9 +373,9 @@
             vmem((2, pieces, gx_size, pad_rows, piece), BF16),
             vmem((2, pieces, gx_size, pad_rows, piece), BF16),
             dma((4,)),
-            dma((-(-total // DEPTH),)),
-            dma((2, gx_size)),
-            dma((2, gy_size)),
+            dma((slabs, -(-total // DEPTH))),
+            dma((2, gx_size, slabs)),
+            dma((2, gy_size, slabs)),
             dma((2, gy_size)),
             dma((2, gy_size * gz_size)),
             dma((2, gx_size * gz_size)),
@@ -368,7 +383,7 @@
             dma((2, 2, pieces, gx_size)),
         ],
         compiler_params=pltpu.CompilerParams(
-            collective_id=0, has_side_effects=True, vmem_limit_bytes=67043328
+            collective_id=0, has_side_effects=True, vmem_limit_bytes=60 * 1024 * 1024
         ),
     )(colloc, occ_coeffs, core.reshape(row_count, flat), place, fold)
     return result[0], result[1]

time: 31.1 us -> 29.6 us (0.952)
  local copies, waits for them, and re-layouts: 1.53 us -> 0.66 us
  Pallas kernels: 28.7 us -> 28.1 us
    squeeze x1, local copies, waits for them, and re-layouts: 1.53 us -> 0.66 us  [local(): return (result[0], result[1])]
    pallas_call x1, Pallas kernels: 28.7 us -> 28.1 us  [local(): pl.pallas_call(functools.partial(kernel, dims), out_shape=pltpu.VMEM((2,...]
where the time goes in v3:
time: 29.6 us; the launch traced here: 29.4 us
  Pallas kernels  28.1 us (95%)
  local copies, waits for them, and re-layouts  0.66 us (2%)
  between operations  0.64 us (2%)
    pallas_call x1, Pallas kernels, local(): pl.pallas_call(functools.partial(kernel, dims), out_shape=pltpu.VMEM((2,...  28.1 us
    squeeze x1, local copies, waits for them, and re-layouts, local(): return (result[0], result[1])  0.66 us

profile of v3, /device:TPU:0, one launch (start us, length us, event | category | flops | bytes accessed | tf_op | source)
XLA Modules:
  0.0 29.4 jit_solution(13241526678098003760)
XLA Ops:
  0.6 28.1 %shard_map.68 = f32[2,6,2000]{2,1,0:T(8,128)S(1)} custom-call(bf16[96,4000]{1,0:T(8,128)(2,1)} %colloc_hbm.1, bf16[4000,256]{1,0:T(8,128)(2,1)} %coeffs_hbm.1, bf16[192,384]{1,0:T(8,128)(2,1)} %bitcast.5, bf16[128,128]{1,0:T(8,128)(2,1)} %constant.4.clone.place_hbm, bf16[96,32]{1,0:T(8,128)(2,1)} %constant.5.clone.fold_hbm), custom_call_target="tpu_custom_call" | custom-call | tf_op jit(solution)/shard_map/pallas_call | solution.py:350
  28.8 0.7 %slice_bitcast_fusion = (f32[6,2000]{1,0:T(8,128)}, f32[6,2000]{1,0:T(8,128)}) fusion(f32[2,6,2000]{2,1,0:T(8,128)S(1)} %shard_map.68), kind=kLoop, calls=%fused_computation | loop fusion | bytes 192000 | tf_op jit(solution)/shard_map/squeeze | solution.py:389
